TPU v7x, 32 devices: a whole 2x2x4 slice. The times are simulated.
32 devices in a mesh: dp: 8 (over z, x), head: 4 (over y, core).
Axes of the slice: x: 2, y: 2, z: 4, core: 2. Of those that a mesh axis runs over, the one named last changes fastest.
Arguments:
- inputs: bfloat16 [8192, 2048], P('dp'), may hold values from -6 to 6
- lengths: int32 [8], P('dp'), may hold values from 256 to 1024, as said below
- gain_attn: bfloat16 [2048], P('dp'), may hold values from 0.5 to 1.5
- w_query: bfloat16 [2048, 2048], P('dp', 'head'), may hold values from -0.25 to 0.25
- w_key: bfloat16 [2048, 2048], P('dp', 'head'), may hold values from -0.25 to 0.25
- w_value: bfloat16 [2048, 2048], P('dp', 'head'), may hold values from -0.125 to 0.125
- w_slot: bfloat16 [2048, 256], P('dp', 'head'), may hold values from -0.125 to 0.125
- gate_bias: float32 [256], P('head'), may hold values from 0 to 8
- w_out: bfloat16 [2048, 2048], P('head', 'dp'), may hold values from -0.5 to 0.5
- gain_ffn: bfloat16 [2048], P('dp'), may hold values from 0.5 to 1.5
- w_gate: bfloat16 [2048, 5632], P('dp', 'head'), may hold values from -0.125 to 0.125
- w_up: bfloat16 [2048, 5632], P('dp', 'head'), may hold values from -0.125 to 0.125
- w_down: bfloat16 [5632, 2048], P('head', 'dp'), may hold values from -0.078125 to 0.078125
- cotangent: bfloat16 [8192, 2048], P('dp'), may hold values from -6 to 6
Outputs:
- output: bfloat16 [8192, 2048], P('dp')
- grad_inputs: float32 [8192, 2048], P('dp')
- grad_gain_attn: float32 [2048], P('dp')
- grad_w_query: float32 [2048, 2048], P('dp', 'head')
- grad_w_key: float32 [2048, 2048], P('dp', 'head')
- grad_w_value: float32 [2048, 2048], P('dp', 'head')
- grad_w_slot: float32 [2048, 256], P('dp', 'head')
- grad_gate_bias: float32 [256], P('head')
- grad_w_out: float32 [2048, 2048], P('head', 'dp')
- grad_gain_ffn: float32 [2048], P('dp')
- grad_w_gate: float32 [2048, 5632], P('dp', 'head')
- grad_w_up: float32 [2048, 5632], P('dp', 'head')
- grad_w_down: float32 [5632, 2048], P('head', 'dp')
Inputs may be any that keep to these rules, and one draw needn't show every extreme that they name: lengths[s] is the number of valid leading positions of sequence s; some sequence has all 1024 valid.
All inputs are finite; a program needn't handle non-finite values.
Results may differ from a plain program's by a relative error of at most 0.014.
Values may be sent and summed in bfloat16 or wider, within the bound.
A program may use at most 256 MiB of HBM per device.

v0:
```python
import jax
import jax.numpy as jnp
from jax import lax
from jax.sharding import PartitionSpec as P

SPAN = 64
epsilon = 1e-06
damping = 8.0
highest = lax.Precision.HIGHEST


def norm_rows(values, gain):
    factor = lax.rsqrt(jnp.mean(values * values, axis=-1, keepdims=True) + epsilon)
    return values * factor * gain


def swiglu(gate_act, up_act):
    return jax.nn.silu(gate_act) * up_act


def span_step(states, pieces):
    queries, key_rows, value_rows, logdecay, writes = pieces
    state_keys, state_values = states
    rows_count = queries.shape[0]
    cumul = jnp.cumsum(logdecay, axis=0)
    causal = (jnp.arange(rows_count)[:, None] >= jnp.arange(rows_count)[None, :])[:, :, None]
    spread = jnp.where(causal, cumul[:, None, :] - cumul[None, :, :], 0.0)
    weighted = jnp.where(causal, jnp.exp(spread), 0.0) * writes[None, :, :]
    scale_factor = queries.shape[1] ** (-0.5)
    inner_products = jnp.dot(queries, key_rows.T, precision=highest) * scale_factor
    carried = jnp.dot(queries, state_keys.T, precision=highest) * scale_factor
    scores = jnp.exp(cumul) * carried + jnp.einsum(
        "tsj,ts->tj", weighted, inner_products, precision=highest
    )
    slot_probs = jax.nn.softmax(scores, axis=-1)
    mixing = jnp.einsum("tj,tsj->ts", slot_probs, weighted, precision=highest)
    result = jnp.dot(slot_probs * jnp.exp(cumul), state_values, precision=highest) + jnp.dot(
        mixing, value_rows, precision=highest
    )
    last_cumul = cumul[-1]
    tail_weight = jnp.exp(last_cumul[None, :] - cumul) * writes
    new_keys = jnp.exp(last_cumul)[:, None] * state_keys + jnp.dot(
        tail_weight.T, key_rows, precision=highest
    )
    new_values = jnp.exp(last_cumul)[:, None] * state_values + jnp.dot(
        tail_weight.T, value_rows, precision=highest
    )
    return ((new_keys, new_values), result)


def slot_mixer(queries, key_rows, value_rows, gate_logits, valid_mask):
    logdecay = valid_mask[:, None] * jax.nn.log_sigmoid(gate_logits) / damping
    writes = valid_mask[:, None] * (1.0 - jnp.exp(logdecay))
    length = queries.shape[0]
    blocks = length // SPAN

    def blocked(matrix):
        return matrix.reshape(blocks, SPAN, matrix.shape[1])

    start_state = (
        jnp.zeros((gate_logits.shape[1], key_rows.shape[1]), jnp.float32),
        jnp.zeros((gate_logits.shape[1], value_rows.shape[1]), jnp.float32),
    )
    _, outputs = lax.scan(
        jax.checkpoint(span_step),
        start_state,
        (
            blocked(queries),
            blocked(key_rows),
            blocked(value_rows),
            blocked(logdecay),
            blocked(writes),
        ),
    )
    return outputs.reshape(length, value_rows.shape[1]) * valid_mask[:, None]


def matmul_low(left, right):
    return jnp.dot(left, right, preferred_element_type=jnp.float32)


def per_device(
    inputs,
    lengths,
    gain_attn,
    w_query,
    w_key,
    w_value,
    w_slot,
    gate_bias,
    w_out,
    gain_ffn,
    w_gate,
    w_up,
    w_down,
    cotangent,
):
    column_set = (
        lax.all_gather(gain_attn, "dp", axis=0, tiled=True),
        lax.all_gather(gain_ffn, "dp", axis=0, tiled=True),
        lax.all_gather(w_query, "dp", axis=0, tiled=True),
        lax.all_gather(w_key, "dp", axis=0, tiled=True),
        lax.all_gather(w_value, "dp", axis=0, tiled=True),
        lax.all_gather(w_slot, "dp", axis=0, tiled=True),
        lax.all_gather(w_gate, "dp", axis=0, tiled=True),
        lax.all_gather(w_up, "dp", axis=0, tiled=True),
    )
    row_set = (
        lax.all_gather(w_out, "dp", axis=1, tiled=True),
        lax.all_gather(w_down, "dp", axis=1, tiled=True),
    )
    (
        full_gain_attn,
        full_gain_ffn,
        full_query,
        full_key,
        full_value,
        full_slot,
        full_gate,
        full_up,
    ) = column_set
    full_out, full_down = row_set
    rows_in = inputs.astype(jnp.float32)
    length = rows_in.shape[0]
    valid_mask = (jnp.arange(length) < lengths[0]).astype(jnp.float32)
    normed, norm_attn_pull = jax.vjp(norm_rows, rows_in, full_gain_attn.astype(jnp.float32))
    normed_low = normed.astype(jnp.bfloat16)
    queries = matmul_low(normed_low, full_query).astype(jnp.bfloat16)
    key_proj = matmul_low(normed_low, full_key).astype(jnp.bfloat16)
    value_proj = matmul_low(normed_low, full_value).astype(jnp.bfloat16)
    gate_logits = matmul_low(normed_low, full_slot) + gate_bias

    def mixer_local(query_in, key_in, value_in, logit_in):
        return slot_mixer(query_in, key_in, value_in, logit_in, valid_mask)

    mixed, mixer_pull = jax.vjp(
        mixer_local,
        queries.astype(jnp.float32),
        key_proj.astype(jnp.float32),
        value_proj.astype(jnp.float32),
        gate_logits,
    )
    mixed_low = mixed.astype(jnp.bfloat16)
    resid = rows_in + lax.psum(matmul_low(mixed_low, full_out), "head")
    normed2, norm_ffn_pull = jax.vjp(norm_rows, resid, full_gain_ffn.astype(jnp.float32))
    normed2_low = normed2.astype(jnp.bfloat16)
    gate_act = matmul_low(normed2_low, full_gate)
    up_act = matmul_low(normed2_low, full_up)
    hidden, swiglu_pull = jax.vjp(swiglu, gate_act, up_act)
    hidden_low = hidden.astype(jnp.bfloat16)
    output_low = (
        resid
        + lax.psum(matmul_low(hidden_low, full_down).astype(jnp.bfloat16), "head").astype(
            jnp.float32
        )
    ).astype(jnp.bfloat16)
    back_cols = (
        lax.all_gather(w_query, "dp", axis=0, tiled=True),
        lax.all_gather(w_key, "dp", axis=0, tiled=True),
        lax.all_gather(w_value, "dp", axis=0, tiled=True),
        lax.all_gather(w_slot, "dp", axis=0, tiled=True),
        lax.all_gather(w_gate, "dp", axis=0, tiled=True),
        lax.all_gather(w_up, "dp", axis=0, tiled=True),
    )
    back_rows = (
        lax.all_gather(w_out, "dp", axis=1, tiled=True),
        lax.all_gather(w_down, "dp", axis=1, tiled=True),
    )
    full_query, full_key, full_value, full_slot, full_gate, full_up = back_cols
    full_out, full_down = back_rows
    d_hidden = matmul_low(cotangent, full_down.T)
    d_gate, d_up = swiglu_pull(d_hidden)
    d_gate_low = d_gate.astype(jnp.bfloat16)
    d_up_low = d_up.astype(jnp.bfloat16)
    grad_down = matmul_low(hidden_low.T, cotangent)
    grad_gate = matmul_low(normed2_low.T, d_gate_low)
    grad_up = matmul_low(normed2_low.T, d_up_low)
    d_normed2 = lax.psum(
        matmul_low(d_gate_low, full_gate.T) + matmul_low(d_up_low, full_up.T), "head"
    )
    d_resid_norm, grad_gain_ffn = norm_ffn_pull(d_normed2)
    d_resid = cotangent.astype(jnp.float32) + d_resid_norm
    d_attn_low = d_resid.astype(jnp.bfloat16)
    grad_out = matmul_low(mixed_low.T, d_attn_low)
    d_mixed = matmul_low(d_attn_low, full_out.T)
    d_query, d_key, d_value, d_logit = mixer_pull(d_mixed)
    grad_bias_part = jnp.sum(d_logit, axis=0)
    d_query_low = d_query.astype(jnp.bfloat16)
    d_key_low = d_key.astype(jnp.bfloat16)
    d_value_low = d_value.astype(jnp.bfloat16)
    d_logit_low = d_logit.astype(jnp.bfloat16)
    grad_query = matmul_low(normed_low.T, d_query_low)
    grad_key = matmul_low(normed_low.T, d_key_low)
    grad_value = matmul_low(normed_low.T, d_value_low)
    grad_slot = matmul_low(normed_low.T, d_logit_low)
    d_normed_part = (
        matmul_low(d_query_low, full_query.T)
        + matmul_low(d_key_low, full_key.T)
        + matmul_low(d_value_low, full_value.T)
        + matmul_low(d_logit_low, full_slot.T)
    )
    d_normed = lax.psum(d_normed_part.astype(jnp.bfloat16), "head").astype(jnp.float32)
    d_inputs_norm, grad_gain_attn = norm_attn_pull(d_normed)
    grad_inputs = d_resid + d_inputs_norm
    column_grads = (
        lax.psum_scatter(grad_gain_attn, "dp", scatter_dimension=0, tiled=True),
        lax.psum_scatter(grad_gain_ffn, "dp", scatter_dimension=0, tiled=True),
        lax.psum_scatter(grad_query, "dp", scatter_dimension=0, tiled=True),
        lax.psum_scatter(grad_key, "dp", scatter_dimension=0, tiled=True),
        lax.psum_scatter(grad_value, "dp", scatter_dimension=0, tiled=True),
        lax.psum_scatter(grad_slot, "dp", scatter_dimension=0, tiled=True),
        lax.psum_scatter(grad_gate, "dp", scatter_dimension=0, tiled=True),
        lax.psum_scatter(grad_up, "dp", scatter_dimension=0, tiled=True),
    )
    row_grads = (
        lax.psum_scatter(
            grad_out.astype(jnp.bfloat16), "dp", scatter_dimension=1, tiled=True
        ).astype(jnp.float32),
        lax.psum_scatter(
            grad_down.astype(jnp.bfloat16), "dp", scatter_dimension=1, tiled=True
        ).astype(jnp.float32),
    )
    grad_bias = lax.psum(grad_bias_part, "dp")
    return (
        output_low,
        grad_inputs,
        column_grads[0],
        column_grads[2],
        column_grads[3],
        column_grads[4],
        column_grads[5],
        grad_bias,
        row_grads[0],
        column_grads[1],
        column_grads[6],
        column_grads[7],
        row_grads[1],
    )


def solution(mesh):
    in_specs = (
        P("dp", None),
        P("dp"),
        P("dp"),
        P("dp", "head"),
        P("dp", "head"),
        P("dp", "head"),
        P("dp", "head"),
        P("head"),
        P("head", "dp"),
        P("dp"),
        P("dp", "head"),
        P("dp", "head"),
        P("head", "dp"),
        P("dp", None),
    )
    out_specs = (
        P("dp", None),
        P("dp", None),
        P("dp"),
        P("dp", "head"),
        P("dp", "head"),
        P("dp", "head"),
        P("dp", "head"),
        P("head"),
        P("head", "dp"),
        P("dp"),
        P("dp", "head"),
        P("dp", "head"),
        P("head", "dp"),
    )
    return jax.shard_map(
        per_device, mesh=mesh, in_specs=in_specs, out_specs=out_specs, check_vma=False
    )
```

profile of v0, /device:TPU:0, one launch (start us, length us, event | category | flops | bytes accessed | tf_op | source)
XLA Modules:
  0.0 2579.9 jit_solution(14699896438426582661)
XLA Ops:
  13.9 22.4 all-gather
  37.0 31.8 %all_gather.39 = bf16[2048,64]{0,1:T(8,128)(2,1)S(1)} all-gather(bf16[256,64]{0,1:T(8,128)(2,1)S(1)} %copy-done.20), channel_id=1, replica_groups=mesh['dp'=8,'head'=4] {'dp'}, dimensions={0}, use_global_device_ids=true | all-gather | bytes 294912 | tf_op jit(solution)/shard_map/all_gather | solution.py:104
  75.4 5.2 convolution_convert_fusion.3
  80.9 34.3 %all-gather.10.cloned.1.call-done = bf16[2048,512]{1,0:T(8,128)(2,1)} async-done(((bf16[256,512]{1,0:T(8,128)(2,1)}), bf16[2048,512]{1,0:T(8,128)(2,1)}) %all-gather.10.cloned.1.call-update) | async-done | bytes 2097168 | tf_op jit(solution)/shard_map/all_gather | solution.py:102
  115.2 5.2 convolution_convert_fusion.5
  122.0 43.0 %all-gather.12.cloned.1.call-done = bf16[2048,512]{1,0:T(8,128)(2,1)} async-done(((bf16[256,512]{1,0:T(8,128)(2,1)}), bf16[2048,512]{1,0:T(8,128)(2,1)}) %all-gather.12.cloned.1.call-update) | async-done | bytes 2097168 | tf_op jit(solution)/shard_map/all_gather | solution.py:103
  165.0 5.2 convolution_convert_fusion.4
  175.0 216.6 %while.52 = (s32[]{:T(128)}, f32[64,512]{1,0:T(8,128)S(1)}, f32[64,512]{1,0:T(8,128)S(1)}, f32[16,64,512]{2,1,0:T(8,128)}, f32[16,64,512]{2,1,0:T(8,128)}, /*ind...) while((s32[]{:T(128)}, f32[64,512]{1,0:T(8,128)S(1)}, ...), condition=%wide.region_5.6_spmd.clone.clone.clone, body=%wide.region_1.5_spmd.clone.clone.sunk.clone | while | flops 157441920 | bytes 3196303 | solution.py:64
  395.2 7.7 fusion.150
  405.0 18.1 all-gather.1
  423.2 131.2 %all-reduce.9.cloned.1.call-done = f32[1024,2048]{1,0:T(8,128)} async-done(((f32[1024,2048]{1,0:T(8,128)}), f32[1024,2048]{1,0:T(8,128)}) %all-reduce.9.cloned.1.call-update) | async-done | bytes 8388624 | tf_op jit(solution)/shard_map/psum | solution.py:144
  554.4 5.7 multiply_reduce_fusion.7
  566.3 82.7 %all-gather.18.cloned.1.call-done = bf16[2048,1408]{1,0:T(8,128)(2,1)} async-done(((bf16[256,1408]{1,0:T(8,128)(2,1)}), bf16[2048,1408]{1,0:T(8,128)(2,1)}) %all-gather.18.cloned.1.call-update) | async-done | bytes 5767184 | tf_op jit(solution)/shard_map/all_gather | solution.py:105
  649.0 11.9 fusion.151
  660.8 80.8 %all-gather.20.cloned.1.call-done = bf16[2048,1408]{1,0:T(8,128)(2,1)} async-done(((bf16[256,1408]{1,0:T(8,128)(2,1)}), bf16[2048,1408]{1,0:T(8,128)(2,1)}) %all-gather.20.cloned.1.call-update) | async-done | bytes 5767184 | tf_op jit(solution)/shard_map/all_gather | solution.py:106
  741.7 11.7 fusion.152
  753.3 81.7 %all-gather.22.cloned.1.call-done = bf16[1408,2048]{1,0:T(8,128)(2,1)} async-done(((bf16[1408,256]{1,0:T(8,128)(2,1)}), bf16[1408,2048]{1,0:T(8,128)(2,1)}) %all-gather.22.cloned.1.call-update) | async-done | bytes 5767184 | tf_op jit(solution)/shard_map/all_gather | solution.py:110
  835.0 15.6 multiply_convert_fusion.1
  850.6 10.9 fusion.153
  861.5 9.0 convolution_add_fusion.9
  872.6 11.9 convolution_convert_fusion.1
  884.5 137.2 %all-reduce.11.cloned.1.call-done = f32[1024,2048]{1,0:T(8,128)} async-done(((f32[1024,2048]{1,0:T(8,128)}), f32[1024,2048]{1,0:T(8,128)}) %all-reduce.11.cloned.1.call-update) | async-done | bytes 8388624 | tf_op jit(solution)/shard_map/psum | solution.py:178
  1021.7 7.1 multiply_reduce_fusion.5
  1031.2 4.8 fusion.118
  1041.6 429.4 %while.51 = (s32[]{:T(128)}, f32[64,512]{1,0:T(8,128)S(1)}, f32[64,512]{1,0:T(8,128)S(1)}, bf16[16,64,512]{2,1,0:T(8,128)(2,1)S(1)}, bf16[16,64,512]{2,1,0:T(8,1...) while((s32[]{:T(128)}, f32[64,512]{1,0:T(8,128)S(1)}, ...), condition=%wide.region_23.24_spmd.clone.clone, body=%wide.region_11.0_spmd.clone.sunk.clone | while | flops 373932032 | bytes 8373975 | solution.py:64
  1474.0 4.1 fusion.154
  1478.1 5.6 fusion.155
  1483.8 5.6 fusion.156
  1489.4 9.5 add_convert_fusion
  1500.1 7.1 convolution_convert_fusion.2
  1507.2 10.7 convolution_convert_fusion
  1522.0 6.5 fusion.158
  1529.8 6.5 fusion.159
  1536.3 6.5 fusion.157
  1542.9 12.3 fusion.160
  1555.3 12.0 fusion.161
  1569.2 82.9 %all-reduce.13.cloned.1.call-done = (bf16[1024,2048]{1,0:T(8,128)(2,1)}, bf16[1024,2048]{1,0:T(8,128)(2,1)}) async-done(((bf16[1024,2048]{1,0:T(8,128)(2,1)}, bf16[1024,2048]{1,0:T(8,128)(2,1)}), (bf16[1024,2048]{1,0:T(8,128)(2,1)}, bf16[1024,2048]{1,0:T(8,128)(2,1)})) %all-reduce.13.cloned.1.call-update) | async-done | bytes 8388624 | tf_op jit(solution)/shard_map/psum | solution.py:153
  1652.1 5.9 fusion.117
  1658.0 38.1 %all-reduce.3 = (f32[2048]{0:T(1024)S(1)}, f32[64]{0:T(128)}, f32[2048]{0:T(1024)S(1)}) all-reduce(f32[2048]{0:T(1024)S(1)} %get-tuple-element.768, f32[64]{0:T(128)S(1)} %neg.61, f32[2048]{0:T(1024)S(1)} %get-tuple-element.766), channel_id=2, replica_groups=mesh['dp'=8,'head'=4] {'dp'}, use_global_device_ids=true, to_apply=%region_27.28.clone | all-reduce | flops 4160 | bytes 33280
  1697.4 27.4 %reduce-scatter.17.cloned.1.call-done = bf16[512,256]{1,0:T(8,128)(2,1)} async-done(((bf16[512,2048]{1,0:T(8,128)(2,1)}), bf16[512,256]{1,0:T(8,128)(2,1)}) %reduce-scatter.17.cloned.1.call-update) | async-done | bytes 262160 | tf_op jit(solution)/shard_map/reduce_scatter | solution.py:216
  1726.5 17.2 fusion.119
  1743.7 94.6 %reduce-scatter.23.cloned.1.call-done = bf16[1408,256]{1,0:T(8,128)(2,1)} async-done(((bf16[1408,2048]{1,0:T(8,128)(2,1)}), bf16[1408,256]{1,0:T(8,128)(2,1)}) %reduce-scatter.23.cloned.1.call-update) | async-done | bytes 720912 | tf_op jit(solution)/shard_map/reduce_scatter | solution.py:219
  1840.6 64.0 %reduce-scatter.15.cloned.1.call-done = f32[256,64]{0,1:T(8,128)} async-done(((f32[2048,64]{0,1:T(8,128)}), f32[256,64]{0,1:T(8,128)}) %reduce-scatter.15.cloned.1.call-update) | async-done | bytes 65552 | tf_op jit(solution)/shard_map/reduce_scatter | solution.py:211
  1904.6 91.5 %reduce-scatter.11.cloned.1.call-done = f32[256,512]{1,0:T(8,128)} async-done(((f32[2048,512]{1,0:T(8,128)}), f32[256,512]{1,0:T(8,128)}) %reduce-scatter.11.cloned.1.call-update) | async-done | bytes 524304 | tf_op jit(solution)/shard_map/reduce_scatter | solution.py:209
  1996.1 92.0 %reduce-scatter.13.cloned.1.call-done = f32[256,512]{1,0:T(8,128)} async-done(((f32[2048,512]{1,0:T(8,128)}), f32[256,512]{1,0:T(8,128)}) %reduce-scatter.13.cloned.1.call-update) | async-done | bytes 524304 | tf_op jit(solution)/shard_map/reduce_scatter | solution.py:210
  2088.1 92.0 %reduce-scatter.9.cloned.1.call-done = f32[256,512]{1,0:T(8,128)} async-done(((f32[2048,512]{1,0:T(8,128)}), f32[256,512]{1,0:T(8,128)}) %reduce-scatter.9.cloned.1.call-update) | async-done | bytes 524304 | tf_op jit(solution)/shard_map/reduce_scatter | solution.py:208
  2180.1 196.5 %reduce-scatter.19.cloned.1.call-done = f32[256,1408]{1,0:T(8,128)} async-done(((f32[2048,1408]{1,0:T(8,128)}), f32[256,1408]{1,0:T(8,128)}) %reduce-scatter.19.cloned.1.call-update) | async-done | bytes 1441808 | tf_op jit(solution)/shard_map/reduce_scatter | solution.py:212
  2376.6 196.0 %reduce-scatter.21.cloned.1.call-done = f32[256,1408]{1,0:T(8,128)} async-done(((f32[2048,1408]{1,0:T(8,128)}), f32[256,1408]{1,0:T(8,128)}) %reduce-scatter.21.cloned.1.call-update) | async-done | bytes 1441808 | tf_op jit(solution)/shard_map/reduce_scatter | solution.py:213
  (1072 shorter events, 698.8 us)
Async XLA Ops:
  7.2 6.2 copy-start.26
  7.2 29.8 %copy-start.20 = (bf16[256,64]{0,1:T(8,128)(2,1)S(1)}, bf16[256,64]{0,1:T(8,128)(2,1)}, u32[]{:S(2)}) copy-start(bf16[256,64]{0,1:T(8,128)(2,1)} %param.24) | copy-start | bytes 98308
  7.2 68.2 %all-gather.14.cloned.1.call-start = ((), (), s32[]{:S(2)}) async-start(), calls=%async_computation.10 | async-start | bytes 2359296 | tf_op jit(solution)/shard_map/all_gather | solution.py:101
  7.9 107.3 %all-gather.10.cloned.1.call-start = ((), (), s32[]{:S(2)}) async-start(), calls=%async_computation.8 | async-start | bytes 2359296 | tf_op jit(solution)/shard_map/all_gather | solution.py:102
  8.7 156.3 %all-gather.12.cloned.1.call-start = ((), (), s32[]{:S(2)}) async-start(), calls=%async_computation.9 | async-start | bytes 2359296 | tf_op jit(solution)/shard_map/all_gather | solution.py:103
  9.4 385.8 %all-gather.16.cloned.1.call-start = ((), (), s32[]{:S(2)}) async-start(), calls=%async_computation.11 | async-start | bytes 2359296 | tf_op jit(solution)/shard_map/all_gather | solution.py:109
  10.0 544.4 %all-reduce.9.cloned.1.call-start = ((), (), s32[]{:S(2)}) async-start(), calls=%async_computation.12 | async-start | bytes 16777216 | tf_op jit(solution)/shard_map/psum | solution.py:144
  10.1 58.8 %copy-start.1 = (bf16[1024,2048]{1,0:T(8,128)(2,1)S(1)}, bf16[1024,2048]{1,0:T(8,128)(2,1)}, u32[]{:S(2)}) copy-start(bf16[1024,2048]{1,0:T(8,128)(2,1)} %param.18) | copy-start | bytes 12582916
  13.4 55.5 %copy-start.16 = (f32[1024]{0:T(1024)}, f32[1024]{0:T(1024)S(1)}, u32[]{:S(2)}) copy-start(f32[1024]{0:T(1024)S(1)} %fusion.140) | copy-start | bytes 12292
  36.4 32.5 %copy-start.14 = (f32[8,1,256]{2,1,0:T(1,128)}, f32[8,1,256]{2,1,0:T(1,128)S(1)}, u32[]{:S(2)}) copy-start(f32[8,1,256]{2,1,0:T(1,128)S(1)} %convert_element_type.131) | copy-start | bytes 24580
  68.8 1.1 copy-start.8
  68.9 3.1 copy-start.21
  69.9 2.0 copy-start.3
  391.7 11.2 copy-start.5
  402.9 2.2 copy-start.27
  402.9 246.1 %all-gather.18.cloned.1.call-start = ((), (), s32[]{:S(2)}) async-start(), calls=%async_computation.13 | async-start | bytes 6488064 | tf_op jit(solution)/shard_map/all_gather | solution.py:105
  403.5 338.2 %all-gather.20.cloned.1.call-start = ((), (), s32[]{:S(2)}) async-start(), calls=%async_computation.14 | async-start | bytes 6488064 | tf_op jit(solution)/shard_map/all_gather | solution.py:106
  404.2 430.8 %all-gather.22.cloned.1.call-start = ((), (), s32[]{:S(2)}) async-start(), calls=%async_computation.15 | async-start | bytes 6488064 | tf_op jit(solution)/shard_map/all_gather | solution.py:110
  405.0 616.8 %all-reduce.11.cloned.1.call-start = ((), (), s32[]{:S(2)}) async-start(), calls=%async_computation.16 | async-start | bytes 16777216 | tf_op jit(solution)/shard_map/psum | solution.py:178
  560.2 3.4 copy-start
  850.6 10.9 copy-start.30
  850.6 10.9 copy-start.29
  850.6 10.9 copy-start.22
  870.5 781.6 %all-reduce.13.cloned.1.call-start = ((), (), s32[]{:S(2)}) async-start(), calls=%async_computation.25 | async-start | bytes 16777216 | tf_op jit(solution)/shard_map/psum | solution.py:153
  1021.7 8.2 copy-start.4
  1021.7 9.4 copy-start.6
  1031.1 4.8 copy-start.25
  1036.0 4.0 copy-start.2
  1041.6 431.9 %copy-start.10 = (f32[1024,64]{0,1:T(8,128)S(1)}, f32[1024,64]{0,1:T(8,128)}, u32[]{:S(2)}) copy-start(f32[1024,64]{0,1:T(8,128)} %get-tuple-element.870) | copy-start | bytes 786436
  1474.0 4.1 copy-start.11
  1474.0 4.1 copy-start.23
  1478.1 5.7 copy-start.12
  1478.1 5.6 copy-start.24
  1483.8 5.6 copy-start.9
  1498.9 1.2 copy-start.7
  1498.9 225.8 %reduce-scatter.17.cloned.1.call-start = ((), (), s32[]{:S(2)}) async-start(), calls=%async_computation.21 | async-start | bytes 2359296 | tf_op jit(solution)/shard_map/reduce_scatter | solution.py:216
  1507.2 331.1 %reduce-scatter.23.cloned.1.call-start = ((), (), s32[]{:S(2)}) async-start(), calls=%async_computation.24 | async-start | bytes 6488064 | tf_op jit(solution)/shard_map/reduce_scatter | solution.py:219
  1518.0 386.6 %reduce-scatter.15.cloned.1.call-start = ((), (), s32[]{:S(2)}) async-start(), calls=%async_computation.20 | async-start | bytes 589824 | tf_op jit(solution)/shard_map/reduce_scatter | solution.py:211
  1522.0 474.1 %reduce-scatter.11.cloned.1.call-start = ((), (), s32[]{:S(2)}) async-start(), calls=%async_computation.18 | async-start | bytes 4718592 | tf_op jit(solution)/shard_map/reduce_scatter | solution.py:209
  1528.5 1.2 copy-start.13
  1528.6 559.5 %reduce-scatter.13.cloned.1.call-start = ((), (), s32[]{:S(2)}) async-start(), calls=%async_computation.19 | async-start | bytes 4718592 | tf_op jit(solution)/shard_map/reduce_scatter | solution.py:210
  1536.3 643.8 %reduce-scatter.9.cloned.1.call-start = ((), (), s32[]{:S(2)}) async-start(), calls=%async_computation.17 | async-start | bytes 4718592 | tf_op jit(solution)/shard_map/reduce_scatter | solution.py:208
  1542.9 833.7 %reduce-scatter.19.cloned.1.call-start = ((), (), s32[]{:S(2)}) async-start(), calls=%async_computation.22 | async-start | bytes 12976128 | tf_op jit(solution)/shard_map/reduce_scatter | solution.py:212
  1555.3 1017.3 %reduce-scatter.21.cloned.1.call-start = ((), (), s32[]{:S(2)}) async-start(), calls=%async_computation.23 | async-start | bytes 12976128 | tf_op jit(solution)/shard_map/reduce_scatter | solution.py:213
  1567.3 0.7 copy-start.28
  1567.3 84.8 %copy-start.15 = (f32[8,1,256]{2,1,0:T(1,128)S(1)}, f32[8,1,256]{2,1,0:T(1,128)}, u32[]{:S(2)}) copy-start(f32[8,1,256]{2,1,0:T(1,128)} %copy-done.14) | copy-start | bytes 24580
  1567.3 84.8 %copy-start.17 = (f32[1024]{0:T(1024)S(1)}, f32[1024]{0:T(1024)}, u32[]{:S(2)}) copy-start(f32[1024]{0:T(1024)} %copy-done.16) | copy-start | bytes 12292
  1652.1 74.4 %copy-start.19 = (f32[1024]{0:T(1024)S(1)}, f32[1024]{0:T(1024)}, u32[]{:S(2)}) copy-start(f32[1024]{0:T(1024)} %copy-done.18) | copy-start | bytes 12292
  (1 other events, 0.6 us)
Sparse Core Ops, SparseCore 0:
  10.1 54.1 all-gather.13
  66.4 48.7 all-gather.9
  117.4 47.6 all-gather.11
  166.9 48.8 all-gather.15
  403.0 151.3 all-reduce.8
  556.5 92.4 all-gather.17
  651.1 90.4 all-gather.19
  743.7 91.3 all-gather.21
  870.6 151.0 all-reduce.10
  1499.0 153.0 all-reduce.12
  1655.6 69.0 reduce-scatter.16
  1728.3 109.9 reduce-scatter.22
  1842.2 62.3 reduce-scatter.14
  1908.7 87.3 reduce-scatter.10
  2000.1 87.9 reduce-scatter.12
  2092.1 87.9 reduce-scatter.8
  2184.1 192.4 reduce-scatter.18
  2380.6 191.9 reduce-scatter.20
where the time goes:
time: 2590 us; the launch traced here: 2580 us
  waiting for transfers between devices  1530 us (59%)
  matrix products  648 us (25%)
  other arithmetic  155 us (6%)
  local copies, waits for them, and re-layouts  111 us (4%)
  blocking collectives  111 us (4%)
    reduce_scatter x1, waiting for transfers between devices, per_device(): lax.psum_scatter(grad_gate, 'dp', scatter_dimension=0, tiled=True)  197 us
    reduce_scatter x1, waiting for transfers between devices, per_device(): lax.psum_scatter(grad_up, 'dp', scatter_dimension=0, tiled=True)  196 us
    dot_general x24, matrix products, matmul_low(): return jnp.dot(left, right, preferred_element_type=jnp.float32)  191 us
    dot_general x48, matrix products, span_step(): mixing = jnp.einsum('tj,tsj->ts', slot_probs, weighted, precision=highest)  166 us
    psum x1, waiting for transfers between devices, per_device(): lax.psum(matmul_low(d_gate_low, full_gate.T) + matmul_low(d_up_low, full_...  137 us
    psum x1, waiting for transfers between devices, per_device(): resid = rows_in + lax.psum(matmul_low(mixed_low, full_out), 'head')  131 us
    dot_general x32, matrix products, span_step(): jnp.einsum('tsj,ts->tj', weighted, inner_products, precision=highest)  106 us
    reduce_scatter x1, waiting for transfers between devices, per_device(): lax.psum_scatter(grad_down.astype(jnp.bfloat16), 'dp', scatter_dimension=...  94.6 us
  transfers between devices with their start and end apart: 18, of which 16 were waited for; matrix products, arithmetic and copies ran while one was open for 15% of the time, Pallas kernels for 0%

commit v1 on v0

--- a/solution.py
+++ b/solution.py
@@ -95,6 +95,19 @@
     w_down,
     cotangent,
 ):
+
+    def place_the_links(arr, axis_id):
+        q_next = lax.axis_size(axis_id)
+        y, seen_now = (q_next, lax.axis_index(axis_id))
+        r1, piece_now = (arr, 1)
+        while piece_now < y:
+            kept_arr = lax.ppermute(r1, axis_id, [(dev_i, dev_i ^ piece_now) for dev_i in range(y)])
+            g_now = jnp.concatenate([r1, kept_arr], axis=0)
+            block_now = jnp.concatenate([kept_arr, r1], axis=0)
+            r1 = jnp.where(seen_now & piece_now == 0, g_now, block_now)
+            piece_now = 2 * piece_now
+        return r1
+
     column_set = (
         lax.all_gather(gain_attn, "dp", axis=0, tiled=True),
         lax.all_gather(gain_ffn, "dp", axis=0, tiled=True),
@@ -103,7 +116,7 @@
         lax.all_gather(w_value, "dp", axis=0, tiled=True),
         lax.all_gather(w_slot, "dp", axis=0, tiled=True),
         lax.all_gather(w_gate, "dp", axis=0, tiled=True),
-        lax.all_gather(w_up, "dp", axis=0, tiled=True),
+        place_the_links(w_up, "dp"),
     )
     row_set = (
         lax.all_gather(w_out, "dp", axis=1, tiled=True),

time: 2590 us -> 2580 us (level)
  waiting for transfers between devices: 1530 us -> 1480 us
    psum x1, waiting for transfers between devices: 131 us -> 82 us  [per_device(): resid = rows_in + lax.psum(matmul_low(mixed_low, full_out), 'head')]
    all_gather x1, waiting for transfers between devices: 80.8 us -> 52.1 us  [per_device(): lax.all_gather(w_up, 'dp', axis=0, tiled=True)]
  transfers between devices with their start and end apart: 18 -> 21, of which waited for: 16 -> 17; matrix products, arithmetic and copies ran while one was open for 15% -> 16% of each run, Pallas kernels for 0% -> 0%
where the time goes in v1:
time: 2580 us; the launch traced here: 2570 us
  waiting for transfers between devices  1480 us (57%)
  matrix products  655 us (25%)
  other arithmetic  162 us (6%)
  blocking collectives  136 us (5%)
  local copies, waits for them, and re-layouts  111 us (4%)
    dot_general x24, matrix products, matmul_low(): return jnp.dot(left, right, preferred_element_type=jnp.float32)  197 us
    reduce_scatter x1, waiting for transfers between devices, per_device(): lax.psum_scatter(grad_gate, 'dp', scatter_dimension=0, tiled=True)  197 us
    reduce_scatter x1, waiting for transfers between devices, per_device(): lax.psum_scatter(grad_up, 'dp', scatter_dimension=0, tiled=True)  196 us
    dot_general x48, matrix products, span_step(): mixing = jnp.einsum('tj,tsj->ts', slot_probs, weighted, precision=highest)  166 us
    psum x1, waiting for transfers between devices, per_device(): lax.psum(matmul_low(d_gate_low, full_gate.T) + matmul_low(d_up_low, full_...  137 us
    dot_general x32, matrix products, span_step(): jnp.einsum('tsj,ts->tj', weighted, inner_products, precision=highest)  106 us
    all_gather x1, waiting for transfers between devices, per_device(): lax.all_gather(w_gate, 'dp', axis=0, tiled=True)  96.9 us
    reduce_scatter x1, waiting for transfers between devices, per_device(): lax.psum_scatter(grad_down.astype(jnp.bfloat16), 'dp', scatter_dimension=...  94.6 us
  transfers between devices with their start and end apart: 21, of which 17 were waited for; matrix products, arithmetic and copies ran while one was open for 16% of the time, Pallas kernels for 0%

profile of v1, /device:TPU:0, one launch (start us, length us, event | category | flops | bytes accessed | tf_op | source)
XLA Modules:
  0.0 2571.7 jit_solution(12144675121116304039)
XLA Ops:
  13.9 22.4 all-gather
  37.0 31.8 %all_gather.38 = bf16[2048,64]{0,1:T(8,128)(2,1)S(1)} all-gather(bf16[256,64]{0,1:T(8,128)(2,1)S(1)} %copy-done.21), channel_id=1, replica_groups=mesh['dp'=8,'head'=4] {'dp'}, dimensions={0}, use_global_device_ids=true | all-gather | bytes 294912 | tf_op jit(solution)/shard_map/all_gather | solution.py:117
  75.4 5.2 convolution_convert_fusion.3
  80.9 34.4 %all-gather.10.cloned.1.call-done = bf16[2048,512]{1,0:T(8,128)(2,1)} async-done(((bf16[256,512]{1,0:T(8,128)(2,1)}), bf16[2048,512]{1,0:T(8,128)(2,1)}) %all-gather.10.cloned.1.call-update) | async-done | bytes 2097168 | tf_op jit(solution)/shard_map/all_gather | solution.py:115
  115.3 5.2 convolution_convert_fusion.5
  122.1 43.0 %all-gather.12.cloned.1.call-done = bf16[2048,512]{1,0:T(8,128)(2,1)} async-done(((bf16[256,512]{1,0:T(8,128)(2,1)}), bf16[2048,512]{1,0:T(8,128)(2,1)}) %all-gather.12.cloned.1.call-update) | async-done | bytes 2097168 | tf_op jit(solution)/shard_map/all_gather | solution.py:116
  165.1 5.2 convolution_convert_fusion.4
  175.1 216.2 %while.52 = (s32[]{:T(128)}, f32[64,512]{1,0:T(8,128)S(1)}, f32[64,512]{1,0:T(8,128)S(1)}, f32[16,64,512]{2,1,0:T(8,128)}, f32[16,64,512]{2,1,0:T(8,128)}, /*ind...) while((s32[]{:T(128)}, f32[64,512]{1,0:T(8,128)S(1)}, ...), condition=%wide.region_5.6_spmd.clone.clone.clone, body=%wide.region_1.5_spmd.clone.clone.sunk.clone | while | flops 157441920 | bytes 3196303 | solution.py:64
  394.8 7.7 fusion.158
  404.6 15.5 collective-permute-done
  424.3 43.3 %all-gather.1 = bf16[8,1,256]{2,1,0:T(2,128)(2,1)S(1)} all-gather(bf16[1,1,256]{2,1,0:T(2,128)(2,1)S(1)} %reshape.298), channel_id=1, replica_groups=mesh['dp'=8,'head'=4] {'dp'}, dimensions={0}, use_global_device_ids=true | all-gather | bytes 4608 | tf_op jit(solution)/shard_map/all_gather | solution.py:113
  472.1 82.0 %all-reduce.9.cloned.1.call-done = f32[1024,2048]{1,0:T(8,128)} async-done(((f32[1024,2048]{1,0:T(8,128)}), f32[1024,2048]{1,0:T(8,128)}) %all-reduce.9.cloned.1.call-update) | async-done | bytes 8388624 | tf_op jit(solution)/shard_map/psum | solution.py:157
  554.1 5.7 multiply_reduce_fusion.7
  565.9 96.9 %all-gather.18.cloned.1.call-done = bf16[2048,1408]{1,0:T(8,128)(2,1)} async-done(((bf16[256,1408]{1,0:T(8,128)(2,1)}), bf16[2048,1408]{1,0:T(8,128)(2,1)}) %all-gather.18.cloned.1.call-update) | async-done | bytes 5767184 | tf_op jit(solution)/shard_map/all_gather | solution.py:118
  662.8 11.9 fusion.159
  674.7 82.3 %all-gather.20.cloned.1.call-done = bf16[1408,2048]{1,0:T(8,128)(2,1)} async-done(((bf16[1408,256]{1,0:T(8,128)(2,1)}), bf16[1408,2048]{1,0:T(8,128)(2,1)}) %all-gather.20.cloned.1.call-update) | async-done | bytes 5767184 | tf_op jit(solution)/shard_map/all_gather | solution.py:123
  757.0 11.8 fusion.160
  768.8 17.3 multiply_convert_fusion.1
  786.0 11.5 fusion.161
  797.6 52.1 %all-gather.22.cloned.1.call-done = bf16[2048,1408]{1,0:T(8,128)(2,1)} async-done(((bf16[256,1408]{1,0:T(8,128)(2,1)}), bf16[2048,1408]{1,0:T(8,128)(2,1)}) %all-gather.22.cloned.1.call-update) | async-done | bytes 5767184 | tf_op jit(solution)/shard_map/all_gather | solution.py:176
  849.7 13.1 convolution_add_fusion.9
  864.9 11.6 convolution_convert_fusion.1
  876.6 137.5 %all-reduce.11.cloned.1.call-done = f32[1024,2048]{1,0:T(8,128)} async-done(((f32[1024,2048]{1,0:T(8,128)}), f32[1024,2048]{1,0:T(8,128)}) %all-reduce.11.cloned.1.call-update) | async-done | bytes 8388624 | tf_op jit(solution)/shard_map/psum | solution.py:191
  1014.1 7.1 multiply_reduce_fusion.5
  1023.5 4.8 fusion.118
  1033.9 429.3 %while.51 = (s32[]{:T(128)}, f32[64,512]{1,0:T(8,128)S(1)}, f32[64,512]{1,0:T(8,128)S(1)}, bf16[16,64,512]{2,1,0:T(8,128)(2,1)S(1)}, bf16[16,64,512]{2,1,0:T(8,1...) while((s32[]{:T(128)}, f32[64,512]{1,0:T(8,128)S(1)}, ...), condition=%wide.region_23.24_spmd.clone.clone, body=%wide.region_11.23_spmd.clone.sunk.clone | while | flops 373932032 | bytes 8373975 | solution.py:64
  1470.2 5.6 fusion.163
  1475.9 5.6 fusion.164
  1481.5 9.5 add_convert_fusion
  1492.2 7.0 convolution_convert_fusion.2
  1499.3 10.9 convolution_convert_fusion
  1514.3 6.5 fusion.166
  1522.1 6.5 fusion.167
  1528.6 6.5 fusion.165
  1535.2 12.2 fusion.168
  1547.5 12.0 fusion.169
  1561.4 82.7 %all-reduce.13.cloned.1.call-done = (bf16[1024,2048]{1,0:T(8,128)(2,1)}, bf16[1024,2048]{1,0:T(8,128)(2,1)}) async-done(((bf16[1024,2048]{1,0:T(8,128)(2,1)}, bf16[1024,2048]{1,0:T(8,128)(2,1)}), (bf16[1024,2048]{1,0:T(8,128)(2,1)}, bf16[1024,2048]{1,0:T(8,128)(2,1)})) %all-reduce.13.cloned.1.call-update) | async-done | bytes 8388624 | tf_op jit(solution)/shard_map/psum | solution.py:166
  1644.1 5.9 fusion.117
  1650.0 38.1 %all-reduce.3 = (f32[2048]{0:T(1024)S(1)}, f32[64]{0:T(128)}, f32[2048]{0:T(1024)S(1)}) all-reduce(f32[2048]{0:T(1024)S(1)} %get-tuple-element.768, f32[64]{0:T(128)S(1)} %neg.61, f32[2048]{0:T(1024)S(1)} %get-tuple-element.766), channel_id=2, replica_groups=mesh['dp'=8,'head'=4] {'dp'}, use_global_device_ids=true, to_apply=%region_27.28.clone | all-reduce | flops 4160 | bytes 33280
  1689.4 27.4 %reduce-scatter.17.cloned.1.call-done = bf16[512,256]{1,0:T(8,128)(2,1)} async-done(((bf16[512,2048]{1,0:T(8,128)(2,1)}), bf16[512,256]{1,0:T(8,128)(2,1)}) %reduce-scatter.17.cloned.1.call-update) | async-done | bytes 262160 | tf_op jit(solution)/shard_map/reduce_scatter | solution.py:229
  1718.6 17.2 fusion.119
  1735.7 94.6 %reduce-scatter.23.cloned.1.call-done = bf16[1408,256]{1,0:T(8,128)(2,1)} async-done(((bf16[1408,2048]{1,0:T(8,128)(2,1)}), bf16[1408,256]{1,0:T(8,128)(2,1)}) %reduce-scatter.23.cloned.1.call-update) | async-done | bytes 720912 | tf_op jit(solution)/shard_map/reduce_scatter | solution.py:232
  1832.7 64.0 %reduce-scatter.15.cloned.1.call-done = f32[256,64]{0,1:T(8,128)} async-done(((f32[2048,64]{0,1:T(8,128)}), f32[256,64]{0,1:T(8,128)}) %reduce-scatter.15.cloned.1.call-update) | async-done | bytes 65552 | tf_op jit(solution)/shard_map/reduce_scatter | solution.py:224
  1896.7 91.5 %reduce-scatter.11.cloned.1.call-done = f32[256,512]{1,0:T(8,128)} async-done(((f32[2048,512]{1,0:T(8,128)}), f32[256,512]{1,0:T(8,128)}) %reduce-scatter.11.cloned.1.call-update) | async-done | bytes 524304 | tf_op jit(solution)/shard_map/reduce_scatter | solution.py:222
  1988.1 92.0 %reduce-scatter.13.cloned.1.call-done = f32[256,512]{1,0:T(8,128)} async-done(((f32[2048,512]{1,0:T(8,128)}), f32[256,512]{1,0:T(8,128)}) %reduce-scatter.13.cloned.1.call-update) | async-done | bytes 524304 | tf_op jit(solution)/shard_map/reduce_scatter | solution.py:223
  2080.1 92.0 %reduce-scatter.9.cloned.1.call-done = f32[256,512]{1,0:T(8,128)} async-done(((f32[2048,512]{1,0:T(8,128)}), f32[256,512]{1,0:T(8,128)}) %reduce-scatter.9.cloned.1.call-update) | async-done | bytes 524304 | tf_op jit(solution)/shard_map/reduce_scatter | solution.py:221
  2172.2 196.5 %reduce-scatter.19.cloned.1.call-done = f32[256,1408]{1,0:T(8,128)} async-done(((f32[2048,1408]{1,0:T(8,128)}), f32[256,1408]{1,0:T(8,128)}) %reduce-scatter.19.cloned.1.call-update) | async-done | bytes 1441808 | tf_op jit(solution)/shard_map/reduce_scatter | solution.py:225
  2368.7 196.0 %reduce-scatter.21.cloned.1.call-done = f32[256,1408]{1,0:T(8,128)} async-done(((f32[2048,1408]{1,0:T(8,128)}), f32[256,1408]{1,0:T(8,128)}) %reduce-scatter.21.cloned.1.call-update) | async-done | bytes 1441808 | tf_op jit(solution)/shard_map/reduce_scatter | solution.py:226
  (1076 shorter events, 711.4 us)
Async XLA Ops:
  7.2 6.2 copy-start.26
  7.2 29.8 %copy-start.21 = (bf16[256,64]{0,1:T(8,128)(2,1)S(1)}, bf16[256,64]{0,1:T(8,128)(2,1)}, u32[]{:S(2)}) copy-start(bf16[256,64]{0,1:T(8,128)(2,1)} %param.24) | copy-start | bytes 98308
  7.2 68.2 %all-gather.14.cloned.1.call-start = ((), (), s32[]{:S(2)}) async-start(), calls=%async_computation.10 | async-start | bytes 2359296 | tf_op jit(solution)/shard_map/all_gather | solution.py:114
  7.9 107.3 %all-gather.10.cloned.1.call-start = ((), (), s32[]{:S(2)}) async-start(), calls=%async_computation.8 | async-start | bytes 2359296 | tf_op jit(solution)/shard_map/all_gather | solution.py:115
  8.7 156.4 %all-gather.12.cloned.1.call-start = ((), (), s32[]{:S(2)}) async-start(), calls=%async_computation.9 | async-start | bytes 2359296 | tf_op jit(solution)/shard_map/all_gather | solution.py:116
  9.4 385.4 %all-gather.16.cloned.1.call-start = ((), (), s32[]{:S(2)}) async-start(), calls=%async_computation.11 | async-start | bytes 2359296 | tf_op jit(solution)/shard_map/all_gather | solution.py:122
  10.0 544.1 %all-reduce.9.cloned.1.call-start = ((), (), s32[]{:S(2)}) async-start(), calls=%async_computation.12 | async-start | bytes 16777216 | tf_op jit(solution)/shard_map/psum | solution.py:157
  10.1 58.8 %copy-start.1 = (bf16[1024,2048]{1,0:T(8,128)(2,1)S(1)}, bf16[1024,2048]{1,0:T(8,128)(2,1)}, u32[]{:S(2)}) copy-start(bf16[1024,2048]{1,0:T(8,128)(2,1)} %param.18) | copy-start | bytes 12582916
  13.4 55.5 %copy-start.17 = (f32[1024]{0:T(1024)}, f32[1024]{0:T(1024)S(1)}, u32[]{:S(2)}) copy-start(f32[1024]{0:T(1024)S(1)} %fusion.147) | copy-start | bytes 12292
  36.4 32.5 %copy-start.15 = (f32[8,1,256]{2,1,0:T(1,128)}, f32[8,1,256]{2,1,0:T(1,128)S(1)}, u32[]{:S(2)}) copy-start(f32[8,1,256]{2,1,0:T(1,128)S(1)} %convert_element_type.131) | copy-start | bytes 24580
  68.8 1.1 copy-start.9
  68.9 3.1 copy-start.22
  69.9 2.0 copy-start.3
  391.3 11.2 copy-start.5
  402.5 1.4 copy-start.8
  402.5 21.8 copy-start.27
  402.5 260.2 %all-gather.18.cloned.1.call-start = ((), (), s32[]{:S(2)}) async-start(), calls=%async_computation.13 | async-start | bytes 6488064 | tf_op jit(solution)/shard_map/all_gather | solution.py:118
  403.1 353.9 %all-gather.20.cloned.1.call-start = ((), (), s32[]{:S(2)}) async-start(), calls=%async_computation.14 | async-start | bytes 6488064 | tf_op jit(solution)/shard_map/all_gather | solution.py:123
  403.9 445.8 %all-gather.22.cloned.1.call-start = ((), (), s32[]{:S(2)}) async-start(), calls=%async_computation.15 | async-start | bytes 6488064 | tf_op jit(solution)/shard_map/all_gather | solution.py:176
  403.9 16.2 collective-permute-start
  421.8 45.9 %collective-permute-start.1 = (bf16[512,1408]{1,0:T(8,128)(2,1)S(1)}, bf16[512,1408]{1,0:T(8,128)(2,1)}, u32[]{:S(2)}, u32[]{:S(2)}) collective-permute-start(bf16[512,1408]{1,0:T(8,128)(2,1)S(1)} %maximum_select_fusion.3), channel_id=1, source_target_pairs={{0,8},{4,12},{8,0},{12,4},{16,24},{20,28},{24,16},{28,20},{1,9},{5... | collective-permute-start | bytes 4325384 | tf_op jit(solution)/shard_map/ppermute | solution.py:104
  424.3 589.8 %all-reduce.11.cloned.1.call-start = ((), (), s32[]{:S(2)}) async-start(), calls=%async_computation.16 | async-start | bytes 16777216 | tf_op jit(solution)/shard_map/psum | solution.py:191
  472.1 296.7 %collective-permute-start.2 = (bf16[1024,1408]{1,0:T(8,128)(2,1)}, bf16[1024,1408]{1,0:T(8,128)(2,1)}, u32[]{:S(2)}, u32[]{:S(2)}) collective-permute-start(bf16[1024,1408]{1,0:T(8,128)(2,1)} %maximum_select_fusion.2), channel_id=1, source_target_pairs={{0,16},{4,20},{8,24},{12,28},{16,0},{20,4},{24,8},{28,12},{1,17},{... | collective-permute-start | bytes 8650760 | tf_op jit(solution)/shard_map/ppermute | solution.py:104
  559.8 3.4 copy-start
  862.8 781.3 %all-reduce.13.cloned.1.call-start = ((), (), s32[]{:S(2)}) async-start(), calls=%async_computation.25 | async-start | bytes 16777216 | tf_op jit(solution)/shard_map/psum | solution.py:166
  1014.1 8.2 copy-start.4
  1014.1 9.4 copy-start.6
  1023.5 4.8 copy-start.25
  1028.3 3.9 copy-start.2
  1033.9 431.8 %copy-start.11 = (f32[1024,64]{0,1:T(8,128)S(1)}, f32[1024,64]{0,1:T(8,128)}, u32[]{:S(2)}) copy-start(f32[1024,64]{0,1:T(8,128)} %get-tuple-element.870) | copy-start | bytes 786436
  1466.1 4.1 copy-start.12
  1466.1 4.1 copy-start.23
  1470.2 5.7 copy-start.13
  1470.2 5.6 copy-start.24
  1475.9 5.6 copy-start.10
  1491.0 1.2 copy-start.7
  1491.0 225.8 %reduce-scatter.17.cloned.1.call-start = ((), (), s32[]{:S(2)}) async-start(), calls=%async_computation.21 | async-start | bytes 2359296 | tf_op jit(solution)/shard_map/reduce_scatter | solution.py:229
  1499.3 331.1 %reduce-scatter.23.cloned.1.call-start = ((), (), s32[]{:S(2)}) async-start(), calls=%async_computation.24 | async-start | bytes 6488064 | tf_op jit(solution)/shard_map/reduce_scatter | solution.py:232
  1510.3 386.4 %reduce-scatter.15.cloned.1.call-start = ((), (), s32[]{:S(2)}) async-start(), calls=%async_computation.20 | async-start | bytes 589824 | tf_op jit(solution)/shard_map/reduce_scatter | solution.py:224
  1514.3 473.8 %reduce-scatter.11.cloned.1.call-start = ((), (), s32[]{:S(2)}) async-start(), calls=%async_computation.18 | async-start | bytes 4718592 | tf_op jit(solution)/shard_map/reduce_scatter | solution.py:222
  1520.8 1.2 copy-start.14
  1520.9 559.3 %reduce-scatter.13.cloned.1.call-start = ((), (), s32[]{:S(2)}) async-start(), calls=%async_computation.19 | async-start | bytes 4718592 | tf_op jit(solution)/shard_map/reduce_scatter | solution.py:223
  1528.6 643.6 %reduce-scatter.9.cloned.1.call-start = ((), (), s32[]{:S(2)}) async-start(), calls=%async_computation.17 | async-start | bytes 4718592 | tf_op jit(solution)/shard_map/reduce_scatter | solution.py:221
  1535.2 833.5 %reduce-scatter.19.cloned.1.call-start = ((), (), s32[]{:S(2)}) async-start(), calls=%async_computation.22 | async-start | bytes 12976128 | tf_op jit(solution)/shard_map/reduce_scatter | solution.py:225
  1547.5 1017.2 %reduce-scatter.21.cloned.1.call-start = ((), (), s32[]{:S(2)}) async-start(), calls=%async_computation.23 | async-start | bytes 12976128 | tf_op jit(solution)/shard_map/reduce_scatter | solution.py:226
  1559.5 84.6 %copy-start.16 = (f32[8,1,256]{2,1,0:T(1,128)S(1)}, f32[8,1,256]{2,1,0:T(1,128)}, u32[]{:S(2)}) copy-start(f32[8,1,256]{2,1,0:T(1,128)} %copy-done.15) | copy-start | bytes 24580
  1559.5 84.6 %copy-start.18 = (f32[1024]{0:T(1024)S(1)}, f32[1024]{0:T(1024)}, u32[]{:S(2)}) copy-start(f32[1024]{0:T(1024)} %copy-done.17) | copy-start | bytes 12292
  1644.1 74.4 %copy-start.20 = (f32[1024]{0:T(1024)S(1)}, f32[1024]{0:T(1024)}, u32[]{:S(2)}) copy-start(f32[1024]{0:T(1024)} %copy-done.19) | copy-start | bytes 12292
  (2 other events, 1.2 us)
Sparse Core Ops, SparseCore 0:
  10.1 54.1 all-gather.13
  66.4 48.7 all-gather.9
  117.4 47.6 all-gather.11
  167.0 48.8 all-gather.15
  402.6 151.4 all-reduce.8
  556.1 106.5 all-gather.17
  664.8 92.1 all-gather.19
  759.2 90.4 all-gather.21
  863.0 151.0 all-reduce.10
  1491.1 152.9 all-reduce.12
  1647.7 69.0 reduce-scatter.16
  1720.3 109.9 reduce-scatter.22
  1834.3 62.3 reduce-scatter.14
  1900.7 87.3 reduce-scatter.10
  1992.2 87.9 reduce-scatter.12
  2084.2 87.9 reduce-scatter.8
  2176.2 192.4 reduce-scatter.18
  2372.7 191.9 reduce-scatter.20
